TPU v7x, 512 devices: a whole 4x4x16 slice. The times are simulated.
512 devices in a mesh: owner: 128 (over x, z, core), replica: 4 (over y).
Axes of the slice: x: 4, y: 4, z: 16, core: 2. Of those that a mesh axis runs over, the one named last changes fastest.
Arguments:
- features: bfloat16 [32768, 4096], P('owner', 'replica'), may hold values from -6 to 6
- cotangent: bfloat16 [32768, 64], P('owner'), may hold values from -0.59765625 to 0.59765625
- adapter_ids: int32 [32768, 1], P('owner'), may hold values from 0 to 255; in each aligned block of 256 rows (0 to 255, 256 to 511, ...) at most 2 rows name the same one
- slot_of: int32 [256], replicated, may hold values from 0 to 255, each once
- active_ids: int32 [192], replicated, may hold values from 0 to 255, as said below
- step_counts: int32 [256], P('owner'), may hold values from 0 to 15
- weight: bfloat16 [256, 64, 4096], P('owner', None, 'replica'), may hold values from -0.09375 to 0.09375
- m_code: bfloat16 [256, 64, 4096], P('owner', None, 'replica'), may hold values from -1 to 1
- m_scale: float32 [256, 32, 4], P('owner', None, 'replica'), may hold values from 0.1 to 1
- v_code: bfloat16 [256, 64, 4096], P('owner', None, 'replica'), may hold values from 0.099609375 to 1
- v_scale: float32 [256, 32, 4], P('owner', None, 'replica'), may hold values from 0.1 to 2
Outputs:
- direction: float32 [256, 64, 4096], P('owner', None, 'replica')
- m_code_new: bfloat16 [256, 64, 4096], P('owner', None, 'replica')
- m_scale_new: float32 [256, 32, 4], P('owner', None, 'replica')
- v_code_new: bfloat16 [256, 64, 4096], P('owner', None, 'replica')
- v_scale_new: float32 [256, 32, 4], P('owner', None, 'replica')
- served: bfloat16 [256, 64, 4096], P('owner')
Inputs may be any that keep to these rules, and one draw needn't show every extreme that they name: `adapter_ids`: among the 256 tokens of one index of owner no adapter is named more than 2 times. `slot_of`: A permutation. `active_ids`: distinct adapters.
All inputs are finite; a program needn't handle non-finite values.
Results may differ from a plain program's by a relative error of at most 0.001.
Values may be sent and summed in bfloat16 or wider, within the bound.
No kernel may reach another device: no remote copies, remote signals or barrier semaphores. Data moves between devices by JAX's collectives and lax.ppermute only.
A program may use at most 64 MiB of HBM per device.

v0:
```python
import functools

import jax
import jax.numpy as jnp
from jax import lax
from jax.experimental import pallas as pl
from jax.experimental.pallas import tpu as pltpu
from jax.sharding import Mesh
from jax.sharding import PartitionSpec as P

beta_one = 0.9
beta_two = 0.999
adam_eps = 1e-08
scale_eps = 1e-06
learn_rate = 0.001
decay_rate = 0.01

LANES = 128
FIRST = 6
VMEM = pl.BlockSpec(memory_space=pltpu.VMEM)
SMEM = pl.BlockSpec(memory_space=pltpu.SMEM)
ANY = pl.BlockSpec(memory_space=pl.ANY)
GRANT = pltpu.CompilerParams(vmem_limit_bytes=16 << 20)


def message_rows(slots, blocks):
    rows = slots * blocks + slots // 2 + 1
    return -(-rows // 4) * 4


def iota(shape, dim):
    return lax.broadcasted_iota(jnp.int32, shape, dim)


def pack_kernel(
    slots, offset, core_ref, owner_ref, ids_ref, slot_ref, act_ref, count_ref, ms_ref, vs_ref, feat_hbm, cot_ref,
    out_ref, aux_ref, scr, feat_ref, feat_sem,
):
    tokens, columns = feat_ref.shape
    rank = cot_ref.shape[0]
    state_rows = slot_ref.shape[1]
    chips, tiles = out_ref.shape[0], out_ref.shape[1]
    rows, blocks = tiles * 4, columns // LANES
    held, pairs = ms_ref.shape
    f32, bf16 = jnp.float32, jnp.bfloat16
    dot = functools.partial(jnp.dot, preferred_element_type=f32)
    here, owner = core_ref[0], owner_ref[0]
    fetch = pltpu.make_async_copy(feat_hbm, feat_ref, feat_sem)
    fetch.start()

    square = (state_rows, state_rows)
    named = slot_ref[...] == iota(square, 0)
    adapter = jnp.sum(jnp.where(named, iota(square, 1), 0).astype(f32), axis=1, keepdims=True)
    adapter = adapter.astype(jnp.int32)
    trained = jnp.max((act_ref[...] == adapter).astype(f32), axis=1, keepdims=True)
    place = jnp.where(ids_ref[...] == adapter, trained, 0.0).astype(bf16)
    of_chip = (iota((chips, state_rows), 1) // 4 == iota((chips, state_rows), 0)).astype(f32).astype(bf16)
    member = dot(of_chip, place)
    earlier = (iota((tokens, tokens), 0) < iota((tokens, tokens), 1)).astype(f32).astype(bf16)
    before = dot(member.astype(bf16), earlier)
    late = jnp.where((member > 0) & (before >= offset + slots), 1.0, 0.0)
    more = jnp.max(jnp.max(late, axis=1, keepdims=True), axis=0, keepdims=True)

    local = (iota((state_rows, LANES), 0) + 2 * here) % 4
    tag = (iota((state_rows, LANES), 1) == rank + local).astype(f32).astype(bf16)
    embed = (iota((rank, LANES), 0) == iota((rank, LANES), 1)).astype(f32).astype(bf16)
    beside = lax.dot_general(
        jnp.concatenate([cot_ref[...], place], axis=0),
        jnp.concatenate([embed, tag], axis=0),
        (((0,), (0,)), ((), ())),
        preferred_element_type=f32,
    )
    chosen = jnp.concatenate(
        [jnp.where(before == offset + i, member, 0.0).astype(bf16) for i in range(slots)], axis=0
    )
    beside = dot(chosen, beside.astype(bf16))
    fetch.wait()
    moved = dot(chosen, feat_ref[...])
    of_slot = [slice(i * chips, (i + 1) * chips) for i in range(slots)]
    for i in range(slots):
        for b in range(blocks):
            scr[pl.ds(i * blocks + b, chips, stride=rows), :] = moved[of_slot[i], b * LANES : (b + 1) * LANES]
    lane = iota((chips, LANES), 1)
    tags = jnp.where(lane == 4 * slots, more, 0.0)
    for i in range(slots):
        one = jnp.where((lane >= rank) & (lane < rank + 4), beside[of_slot[i]], 0.0)
        tags = tags + pltpu.roll(one, (LANES - rank + 4 * i) % LANES, 1)
    for p in range(slots // 2):
        pair = jnp.where(lane < rank, beside[of_slot[2 * p]], pltpu.roll(beside[of_slot[2 * p + 1]], rank, 1))
        scr[pl.ds(slots * blocks + p, chips, stride=rows), :] = pair
    for r in range(slots * blocks + slots // 2, rows):
        scr[pl.ds(r, chips, stride=rows), :] = tags
    out_ref[...] = scr[...].astype(bf16).reshape(chips, tiles, 4, LANES)

    aux_ref[...] = jnp.zeros(aux_ref.shape, f32)
    aux_ref[:held, :pairs] = ms_ref[...]
    aux_ref[held : 2 * held, :pairs] = vs_ref[...]
    count = count_ref[...] + 1
    for at, beta in ((2 * held, beta_one), (2 * held + 1, beta_two)):
        power = jnp.ones(count.shape, f32)
        for bit in range(8):
            power = jnp.where((count >> bit) % 2 == 1, power * beta ** (1 << bit), power)
        aux_ref[at : at + 1, :held] = 1.0 / (1.0 - power)
    state_row = iota((state_rows, held), 0) - held * owner
    mine = jnp.where(state_row == iota((state_rows, held), 1), trained, 0.0)
    aux_ref[2 * held + 2 : 2 * held + 3, :held] = jnp.max(mine, axis=0, keepdims=True)


def pack(slots, offset, core, owner, ids, slot_of, active, counts, m_scale, v_scale, features, cotangent, chips):
    blocks = features.shape[1] // LANES
    rows = message_rows(slots, blocks)
    return pl.pallas_call(
        functools.partial(pack_kernel, slots, offset),
        out_shape=(
            jax.ShapeDtypeStruct((chips, rows // 4, 4, LANES), features.dtype),
            jax.ShapeDtypeStruct((8, LANES), jnp.float32),
        ),
        in_specs=[SMEM, SMEM] + [VMEM] * 6 + [ANY, VMEM],
        out_specs=(VMEM, VMEM),
        scratch_shapes=[
            pltpu.VMEM((chips * rows, LANES), jnp.float32),
            pltpu.VMEM(features.shape, features.dtype),
            pltpu.SemaphoreType.DMA,
        ],
        compiler_params=GRANT,
        name=f"pack{slots}",
    )(core, owner, ids, slot_of, active, counts, m_scale, v_scale, features, cotangent)


def grad_kernel(slots, in_ref, own_ref, other_ref, flag_ref, scr):
    chips, tiles = in_ref.shape[0], in_ref.shape[1]
    rows = tiles * 4
    half, columns = own_ref.shape
    rank = half // 2
    blocks = columns // LANES
    f32, bf16 = jnp.float32, jnp.bfloat16
    scr[...] = in_ref[...].reshape(chips * rows, LANES).astype(f32)
    low = iota((chips, LANES), 1) < rank
    tags = scr[pl.ds(rows - 1, chips, stride=rows), :]
    weights, wide = [], []
    for i in range(slots):
        pair = scr[pl.ds(slots * blocks + i // 2, chips, stride=rows), :]
        one = jnp.where(low if i % 2 == 0 else ~low, pair, 0.0)
        both = one + pltpu.roll(one, rank, 1)
        h = [tags[:, 4 * i + l : 4 * i + l + 1] for l in range(4)]
        weights.append(
            jnp.concatenate(
                [both * jnp.where(low, h[0], h[1]), both * jnp.where(low, h[2], h[3])], axis=1
            ).astype(bf16)
        )
        wide.append(
            jnp.concatenate(
                [scr[pl.ds(i * blocks + b, chips, stride=rows), :] for b in range(blocks)], axis=1
            ).astype(bf16)
        )
    total = lax.dot_general(
        jnp.concatenate(weights, axis=0),
        jnp.concatenate(wide, axis=0),
        (((0,), (0,)), ((), ())),
        preferred_element_type=f32,
    )
    own_ref[...] = total[:half]
    other_ref[:half, :] = total[half:]
    more = jnp.max(tags[:, 4 * slots : 4 * slots + 1], axis=0, keepdims=True)
    other_ref[half:, :] = jnp.broadcast_to(more, (8, columns))
    flag_ref[...] = jnp.broadcast_to(more, flag_ref.shape)


def partial_gradients(slots, received, half, columns):
    chips, tiles = received.shape[0], received.shape[1]
    f32 = jnp.float32
    return pl.pallas_call(
        functools.partial(grad_kernel, slots),
        out_shape=(
            jax.ShapeDtypeStruct((half, columns), f32),
            jax.ShapeDtypeStruct((half + 8, columns), f32),
            jax.ShapeDtypeStruct((8, LANES), f32),
        ),
        in_specs=[VMEM],
        out_specs=(VMEM, VMEM, VMEM),
        scratch_shapes=[pltpu.VMEM((chips * tiles * 4, LANES), f32)],
        compiler_params=GRANT,
        name=f"grad{slots}",
    )(received)


def moments(j, aux_ref, gradient, mc_ref, vc_ref, spread):
    f32 = jnp.float32
    held, rank, _ = mc_ref.shape
    pairs = rank // 2

    def per_row(at):
        return jnp.sum(jnp.where(spread, aux_ref[at : at + 1, :pairs], 0.0), axis=1, keepdims=True)

    moment = mc_ref[j].astype(f32) * (beta_one * per_row(j)) + (1.0 - beta_one) * gradient
    second = vc_ref[j].astype(f32) * (beta_two * per_row(held + j)) + (1.0 - beta_two) * gradient * gradient
    inverse_one = aux_ref[2 * held : 2 * held + 1, j : j + 1]
    inverse_two = aux_ref[2 * held + 1 : 2 * held + 2, j : j + 1]
    direction = (moment * inverse_one) / (jnp.sqrt(second * inverse_two) + adam_eps)
    return moment, second, direction


def row_spread(rank):
    return iota((rank, rank // 2), 0) // 2 == iota((rank, rank // 2), 1)


def trained_row(aux_ref, held, j, shape):
    return jnp.broadcast_to(aux_ref[2 * held + 2 : 2 * held + 3, j : j + 1], shape) > 0


def serve_kernel(
    aux_ref, own_ref, other_ref, flag_ref, weight_ref, mc_ref, vc_ref,
    served_hbm, total_ref, more_ref, out_ref, sems,
):
    held, rank, columns = weight_ref.shape
    spread = row_spread(rank)
    more_ref[...] = flag_ref[...] + other_ref[held * rank :, :LANES]
    sends = []
    for j in range(held):
        at = slice(j * rank, (j + 1) * rank)
        gradient = own_ref[at, :] + other_ref[at, :]
        total_ref[at, :] = gradient
        _, _, direction = moments(j, aux_ref, gradient, mc_ref, vc_ref, spread)
        weight = weight_ref[j].astype(jnp.float32)
        served = weight - learn_rate * (direction + decay_rate * weight)
        served = jnp.where(trained_row(aux_ref, held, j, weight.shape), served, weight)
        out_ref[j] = served.astype(out_ref.dtype)
        for r in range(served_hbm.shape[0]):
            send = pltpu.make_async_copy(out_ref.at[j], served_hbm.at[r, j], sems.at[j, r])
            send.start()
            sends.append(send)
    for send in sends:
        send.wait()


def serve(replicas, aux, own, other, flag, weight, m_code, v_code):
    held = weight.shape[0]
    like = jax.ShapeDtypeStruct
    return pl.pallas_call(
        serve_kernel,
        out_shape=(
            like((replicas, *weight.shape), weight.dtype),
            like(own.shape, jnp.float32),
            like(flag.shape, jnp.float32),
        ),
        in_specs=[VMEM] * 7,
        out_specs=(ANY, VMEM, VMEM),
        scratch_shapes=[
            pltpu.VMEM(weight.shape, weight.dtype),
            pltpu.SemaphoreType.DMA((held, replicas)),
        ],
        compiler_params=GRANT,
        name="serve",
    )(aux, own, other, flag, weight, m_code, v_code)


def state_kernel(
    aux_ref, total_ref, flag_ref, mc_ref, vc_ref, dir_ref, mc_out, ms_out, vc_out, vs_out, more_ref
):
    f32 = jnp.float32
    held, rank, columns = mc_ref.shape
    pairs = rank // 2
    spread = row_spread(rank)

    def per_pair(values):
        return jnp.max(jnp.where(spread, values, 0.0), axis=0, keepdims=True)

    def per_row(scales):
        return jnp.sum(jnp.where(spread, scales, 0.0), axis=1, keepdims=True)

    more_ref[...] = flag_ref[...]
    for j in range(held):
        gradient = total_ref[j * rank : (j + 1) * rank, :]
        moment, second, direction = moments(j, aux_ref, gradient, mc_ref, vc_ref, spread)
        keep = trained_row(aux_ref, held, j, moment.shape)
        keep_row = trained_row(aux_ref, held, j, (1, pairs))
        m_new = per_pair(jnp.max(jnp.abs(moment), axis=1, keepdims=True)) + scale_eps
        v_new = per_pair(jnp.max(second, axis=1, keepdims=True)) + scale_eps
        dir_ref[j] = jnp.where(keep, direction, 0.0)
        m_code, v_code = moment / per_row(m_new), second / per_row(v_new)
        mc_out[j] = jnp.where(keep, m_code, mc_ref[j].astype(f32)).astype(mc_out.dtype)
        vc_out[j] = jnp.where(keep, v_code, vc_ref[j].astype(f32)).astype(vc_out.dtype)
        ms_out[j : j + 1, :] = jnp.where(keep_row, m_new, aux_ref[j : j + 1, :pairs])
        vs_out[j : j + 1, :] = jnp.where(keep_row, v_new, aux_ref[held + j : held + j + 1, :pairs])


def state(aux, total, flag, m_code, v_code):
    f32 = jnp.float32
    like = jax.ShapeDtypeStruct
    scales = like((m_code.shape[0], m_code.shape[1] // 2), f32)
    return pl.pallas_call(
        state_kernel,
        out_shape=(
            like(m_code.shape, f32),
            like(m_code.shape, m_code.dtype),
            scales,
            like(v_code.shape, v_code.dtype),
            scales,
            like(flag.shape, f32),
        ),
        in_specs=[VMEM] * 5,
        out_specs=(VMEM,) * 6,
        compiler_params=GRANT,
        name="state",
    )(aux, total, flag, m_code, v_code)


def on_device(
    features, cotangent, adapter_ids, slot_of, active_ids, step_counts,
    weight, m_code, m_scale, v_code, v_scale,
):
    columns = features.shape[1]
    held, rank = weight.shape[0], weight.shape[1]
    half = held * rank
    chips = lax.axis_size(("x", "z"))
    replicas = lax.axis_size("replica")
    core = lax.axis_index("core").astype(jnp.int32).reshape(1)
    owner = lax.axis_index(("x", "z", "core")).astype(jnp.int32).reshape(1)
    arrays = (
        adapter_ids.reshape(1, -1), slot_of.reshape(1, -1), active_ids.reshape(1, -1), step_counts.reshape(1, -1),
        m_scale.reshape(held, -1), v_scale.reshape(held, -1), features, cotangent.T,
    )
    swap = [(0, 1), (1, 0)]

    def exchange(slots, offset, core):
        sent, aux = pack(slots, offset, core, owner, *arrays, chips)
        received = lax.all_to_all(sent, ("x", "z"), split_axis=0, concat_axis=0, tiled=True)
        own, other, flag = partial_gradients(slots, received, half, columns)
        return own, lax.ppermute(other, "core", swap), flag, aux

    def update(own, other, flag, aux):
        copies, total, more = serve(replicas, aux, own, other, flag, weight, m_code, v_code)
        parts = lax.all_to_all(copies, "replica", split_axis=0, concat_axis=0, tiled=True)
        served = jnp.moveaxis(parts, 0, 2).reshape(held, rank, -1)
        direction, m_new, ms_new, v_new, vs_new, more = state(aux, total, more, m_code, v_code)
        return total, (more[0, 0], direction, m_new, ms_new, v_new, vs_new, served)

    total, results = update(*exchange(FIRST, 0, core))

    def with_the_rest(carry):
        here = core + (carry[0] < 0).astype(jnp.int32)
        own, other, flag, aux = exchange(8 - FIRST, FIRST, here)
        return update(total + own, other, flag, aux)[1]

    results = lax.while_loop(lambda carry: carry[0] > 0, with_the_rest, results)
    _, direction, m_new, ms_new, v_new, vs_new, served = results
    return (
        direction, m_new, ms_new.reshape(m_scale.shape), v_new, vs_new.reshape(v_scale.shape), served,
    )


def solution(mesh):
    owners, replicas = mesh.devices.shape
    fine = Mesh(mesh.devices.reshape(4, owners // 8, 2, replicas), ("x", "z", "core", "replica"))
    owner = ("x", "z", "core")
    block = P(owner, None, "replica")
    return jax.shard_map(
        on_device,
        mesh=fine,
        in_specs=(
            P(owner, "replica"), P(owner, None), P(owner, None), P(), P(), P(owner),
            block, block, block, block, block,
        ),
        out_specs=(block, block, block, block, block, P(owner, None, None)),
        check_vma=False,
    )
```

profile of v0, /device:TPU:6, one launch (start us, length us, event | category | flops | bytes accessed | tf_op | source)
XLA Modules:
  0.0 95.3 jit_solution(278240226536743903)
XLA Ops:
  0.6 0.0 copy-start.4
  0.7 0.0 copy-start.8
  0.7 0.0 copy-start.9
  0.7 0.0 copy-start.6
  0.7 0.0 copy-start.7
  0.7 0.0 copy-start.5
  0.7 0.0 copy-start.10
  0.7 0.7 copy-done.4
  1.4 0.0 copy-done.8
  1.4 0.0 copy-done.9
  1.4 1.7 %pack6.1 = (bf16[64,13,4,128]{3,2,1,0:T(4,128)(2,1)S(1)}, f32[8,128]{1,0:T(8,128)S(1)}) custom-call(s32[1]{0:T(128)} %bitcast.3.core_ref, s32[1]{0:T(128)} %bitcast.4.owner_ref, s32[1,256]{1,0:T(1,128)S(1)} %bitcast.38, s32[1,256]{1,0:T(1,128)S(1)} %bitcast.40, s32[1,192]{1,0:T(1,128)S(1)} %bitcast.42, s32[1,2]{1,0:T(1,128)S(1)} %bitcast.48, ...), custom_call_target="tpu_custom_call" | custom-call | tf_op jit(solution)/shard_map/pack6/pallas_call | solution.py:112
  3.2 64.2 %all_to_all.22.in_ref = bf16[64,13,4,128]{3,2,1,0:T(4,128)(2,1)S(1)} all-to-all(bf16[64,13,4,128]{3,2,1,0:T(4,128)(2,1)S(1)} %get-tuple-element.141), channel_id=1, replica_groups=mesh['x'=4,'z'=16,'core'=2,'replica'=4] {'x','z'}, dimensions={0} | all-to-all | bytes 1703936 | tf_op jit(solution)/shard_map/all_to_all | solution.py:327
  67.3 0.9 grad6.1
  68.2 1.9 %collective-permute-start.1 = (f32[136,1024]{1,0:T(8,128)S(1)}, f32[136,1024]{1,0:T(8,128)S(1)}, u32[]{:S(2)}, u32[]{:S(2)}) collective-permute-start(f32[136,1024]{1,0:T(8,128)S(1)} %get-tuple-element.143), channel_id=1, source_target_pairs={{0,4},{4,0},{1,5},{5,1},{2,6},{6,2},{3,7},{7,3},{8,12},{12,8},{9,1... | collective-permute-start | bytes 1671176 | tf_op jit(solution)/shard_map/ppermute | solution.py:329
  70.1 1.9 %collective-permute-done.1.other_ref = f32[136,1024]{1,0:T(8,128)S(1)} collective-permute-done((f32[136,1024]{1,0:T(8,128)S(1)}, f32[136,1024]{1,0:T(8,128)S(1)}, u32[]{:S(2)}, u32[]{:S(2)}) %collective-permute-start.1) | collective-permute-done | bytes 557088 | tf_op jit(solution)/shard_map/ppermute | solution.py:329
  72.1 0.0 copy-done.1
  72.1 1.5 %serve.2 = (bf16[4,2,64,1024]{3,2,1,0:T(8,128)(2,1)}, f32[128,1024]{1,0:T(8,128)S(1)}, f32[8,128]{1,0:T(8,128)S(1)}) custom-call(f32[8,128]{1,0:T(8,128)S(1)} %get-tuple-element.140.aux_ref, f32[128,1024]{1,0:T(8,128)S(1)} %get-tuple-element.142.own_ref, f32[136,1024]{1,0:T(8,128)S(1)} %collective-permute-done.1.other_ref, ...), custom_call_target="tpu_custom_call" | custom-call | tf_op jit(solution)/shard_map/serve/pallas_call | solution.py:239
  73.5 4.5 %all-to-all-start.3 = ((bf16[4,2,64,1024]{3,2,1,0:T(8,128)(2,1)}), bf16[4,2,64,1024]{3,2,1,0:T(8,128)(2,1)S(1)}, u32[]{:S(2)}, u32[]{:S(2)}) async-start(bf16[4,2,64,1024]{3,2,1,0:T(8,128)(2,1)} %get-tuple-element.153), calls=%async_computation.3 | async-start | bytes 2097152 | tf_op jit(solution)/shard_map/all_to_all | solution.py:333
  78.0 1.7 %state.2 = (f32[2,64,1024]{2,1,0:T(8,128)}, bf16[2,64,1024]{2,1,0:T(8,128)(2,1)}, f32[2,32]{1,0:T(2,128)}, bf16[2,64,1024]{2,1,0:T(8,128)(2,1)}, f32[2,32]{1,0:T(2,128)}, /*index=5*/f32[8,128]{1,0:T(8,128)S(1)}) custom-call(f32[8,128]{1,0:T(8,128)S(1)} %get-tuple-element.140.aux_ref, f32[128,1024]{1,0:T(8,128)S(1)} %get-tuple-element.374.total_ref, ...), custom_call_target="tpu_custom_call" | custom-call | tf_op jit(solution)/shard_map/state/pallas_call | solution.py:291
  79.7 0.6 slice.6
  80.3 13.1 %all-to-all-done.3 = bf16[4,2,64,1024]{3,2,1,0:T(8,128)(2,1)S(1)} async-done(((bf16[4,2,64,1024]{3,2,1,0:T(8,128)(2,1)}), bf16[4,2,64,1024]{3,2,1,0:T(8,128)(2,1)S(1)}, u32[]{:S(2)}, u32[]{:S(2)}) %all-to-all-start.3) | async-done | bytes 1048608 | tf_op jit(solution)/shard_map/all_to_all | solution.py:333
  93.4 1.0 %copy.24 = bf16[4,2,8,8,1024]{4,3,0,2,1:T(8,128)(2,1)} copy(bf16[4,2,8,8,1024]{4,3,2,1,0:T(8,128)(2,1)S(1)} %bitcast.33) | data formatting | bytes 2097152 | tf_op jit(solution)/shard_map/reshape | solution.py:334
  94.4 0.2 copy-done.2
  94.6 0.7 while.20
  (10 shorter events, 0.0 us)
Async XLA Ops:
  0.6 0.8 copy-start.4
  0.7 0.7 copy-start.8
  0.7 0.7 copy-start.9
  0.7 0.7 copy-start.6
  0.7 0.7 copy-start.7
  0.7 0.7 copy-start.5
  0.7 0.7 copy-start.10
  67.3 4.7 %copy-start = (bf16[2,64,1024]{2,1,0:T(8,128)(2,1)S(1)}, bf16[2,64,1024]{2,1,0:T(8,128)(2,1)}, u32[]{:S(2)}) copy-start(bf16[2,64,1024]{2,1,0:T(8,128)(2,1)} %mc_ref.3) | copy-start | bytes 786436
  67.3 4.7 %copy-start.1 = (bf16[2,64,1024]{2,1,0:T(8,128)(2,1)S(1)}, bf16[2,64,1024]{2,1,0:T(8,128)(2,1)}, u32[]{:S(2)}) copy-start(bf16[2,64,1024]{2,1,0:T(8,128)(2,1)} %vc_ref.3) | copy-start | bytes 786436
  67.3 4.7 %copy-start.3 = (bf16[2,64,1024]{2,1,0:T(8,128)(2,1)S(1)}, bf16[2,64,1024]{2,1,0:T(8,128)(2,1)}, u32[]{:S(2)}) copy-start(bf16[2,64,1024]{2,1,0:T(8,128)(2,1)} %weight_ref.1) | copy-start | bytes 786436
  68.2 3.9 %collective-permute-start.1 = (f32[136,1024]{1,0:T(8,128)S(1)}, f32[136,1024]{1,0:T(8,128)S(1)}, u32[]{:S(2)}, u32[]{:S(2)}) collective-permute-start(f32[136,1024]{1,0:T(8,128)S(1)} %get-tuple-element.143), channel_id=1, source_target_pairs={{0,4},{4,0},{1,5},{5,1},{2,6},{6,2},{3,7},{7,3},{8,12},{12,8},{9,1... | collective-permute-start | bytes 1671176 | tf_op jit(solution)/shard_map/ppermute | solution.py:329
  73.5 19.9 %all-to-all-start.3 = ((bf16[4,2,64,1024]{3,2,1,0:T(8,128)(2,1)}), bf16[4,2,64,1024]{3,2,1,0:T(8,128)(2,1)S(1)}, u32[]{:S(2)}, u32[]{:S(2)}) async-start(bf16[4,2,64,1024]{3,2,1,0:T(8,128)(2,1)} %get-tuple-element.153), calls=%async_computation.3 | async-start | bytes 2097152 | tf_op jit(solution)/shard_map/all_to_all | solution.py:333
  93.4 1.2 %copy-start.2 = (bf16[256,1024]{1,0:T(8,128)(2,1)S(1)}, bf16[256,1024]{1,0:T(8,128)(2,1)}, u32[]{:S(2)}) copy-start(bf16[256,1024]{1,0:T(8,128)(2,1)} %feat_hbm.1) | copy-start | bytes 1572868
where the time goes:
time: 95.7 us; the launch traced here: 95.3 us
  blocking collectives  64.2 us (67%)
  waiting for transfers between devices  15 us (16%)
  starting transfers between devices  6.4 us (7%)
  Pallas kernels  5.76 us (6%)
  local copies, waits for them, and re-layouts  2.51 us (3%)
    all_to_all x1, blocking collectives, exchange(): lax.all_to_all(sent, ('x', 'z'), split_axis=0, concat_axis=0, tiled=True)  64.2 us
    all_to_all x1, waiting for transfers between devices, update(): lax.all_to_all(copies, 'replica', split_axis=0, concat_axis=0, tiled=True)  13.1 us
    all_to_all x1, starting transfers between devices, update(): lax.all_to_all(copies, 'replica', split_axis=0, concat_axis=0, tiled=True)  4.48 us
    ppermute x1, waiting for transfers between devices, exchange(): return (own, lax.ppermute(other, 'core', swap), flag, aux)  1.92 us
    ppermute x1, starting transfers between devices, exchange(): return (own, lax.ppermute(other, 'core', swap), flag, aux)  1.92 us
  transfers between devices with their start and end apart: 2, of which 2 were waited for; matrix products, arithmetic and copies ran while one was open for 1% of the time, Pallas kernels for 2%

commit v1 on v0

--- a/solution.py
+++ b/solution.py
@@ -24,7 +24,7 @@
 
 
 def message_rows(slots, blocks):
-    rows = slots * blocks + slots // 2 + 1
+    rows = slots * blocks + (slots + 1) // 2 + 1
     return -(-rows // 4) * 4
 
 
@@ -33,20 +33,20 @@
 
 
 def pack_kernel(
-    slots, offset, core_ref, owner_ref, ids_ref, slot_ref, act_ref, count_ref, ms_ref, vs_ref, feat_hbm, cot_ref,
+    slots, core_ref, owner_ref, offset_ref, ids_ref, slot_ref, act_ref, count_ref, ms_ref, vs_ref, cot_ref, feat_hbm,
     out_ref, aux_ref, scr, feat_ref, feat_sem,
 ):
-    tokens, columns = feat_ref.shape
-    rank = cot_ref.shape[0]
+    fetch = pltpu.make_async_copy(feat_hbm, feat_ref, feat_sem)
+    fetch.start()
+    rank, tokens = cot_ref.shape
     state_rows = slot_ref.shape[1]
+    columns = feat_ref.shape[1]
     chips, tiles = out_ref.shape[0], out_ref.shape[1]
     rows, blocks = tiles * 4, columns // LANES
     held, pairs = ms_ref.shape
     f32, bf16 = jnp.float32, jnp.bfloat16
     dot = functools.partial(jnp.dot, preferred_element_type=f32)
-    here, owner = core_ref[0], owner_ref[0]
-    fetch = pltpu.make_async_copy(feat_hbm, feat_ref, feat_sem)
-    fetch.start()
+    here, owner, offset = core_ref[0], owner_ref[0], offset_ref[0].astype(f32)
 
     square = (state_rows, state_rows)
     named = slot_ref[...] == iota(square, 0)
@@ -57,9 +57,10 @@
     of_chip = (iota((chips, state_rows), 1) // 4 == iota((chips, state_rows), 0)).astype(f32).astype(bf16)
     member = dot(of_chip, place)
     earlier = (iota((tokens, tokens), 0) < iota((tokens, tokens), 1)).astype(f32).astype(bf16)
-    before = dot(member.astype(bf16), earlier)
-    late = jnp.where((member > 0) & (before >= offset + slots), 1.0, 0.0)
+    before = dot(member.astype(bf16), earlier) - offset
+    late = jnp.where((member > 0) & (before >= slots), 1.0, 0.0)
     more = jnp.max(jnp.max(late, axis=1, keepdims=True), axis=0, keepdims=True)
+    chosen = jnp.concatenate([jnp.where(before == i, member, 0.0).astype(bf16) for i in range(slots)], axis=0)
 
     local = (iota((state_rows, LANES), 0) + 2 * here) % 4
     tag = (iota((state_rows, LANES), 1) == rank + local).astype(f32).astype(bf16)
@@ -69,9 +70,6 @@
         jnp.concatenate([embed, tag], axis=0),
         (((0,), (0,)), ((), ())),
         preferred_element_type=f32,
-    )
-    chosen = jnp.concatenate(
-        [jnp.where(before == offset + i, member, 0.0).astype(bf16) for i in range(slots)], axis=0
     )
     beside = dot(chosen, beside.astype(bf16))
     fetch.wait()
@@ -85,12 +83,14 @@
     for i in range(slots):
         one = jnp.where((lane >= rank) & (lane < rank + 4), beside[of_slot[i]], 0.0)
         tags = tags + pltpu.roll(one, (LANES - rank + 4 * i) % LANES, 1)
-    for p in range(slots // 2):
-        pair = jnp.where(lane < rank, beside[of_slot[2 * p]], pltpu.roll(beside[of_slot[2 * p + 1]], rank, 1))
+    for p in range((slots + 1) // 2):
+        pair = jnp.where(lane < rank, beside[of_slot[2 * p]], 0.0)
+        if 2 * p + 1 < slots:
+            pair = jnp.where(lane < rank, pair, pltpu.roll(beside[of_slot[2 * p + 1]], rank, 1))
         scr[pl.ds(slots * blocks + p, chips, stride=rows), :] = pair
-    for r in range(slots * blocks + slots // 2, rows):
+    for r in range(slots * blocks + (slots + 1) // 2, rows):
         scr[pl.ds(r, chips, stride=rows), :] = tags
-    out_ref[...] = scr[...].astype(bf16).reshape(chips, tiles, 4, LANES)
+    out_ref[...] = scr[...].astype(out_ref.dtype).reshape(chips, tiles, 4, LANES)
 
     aux_ref[...] = jnp.zeros(aux_ref.shape, f32)
     aux_ref[:held, :pairs] = ms_ref[...]
@@ -106,16 +106,13 @@
     aux_ref[2 * held + 2 : 2 * held + 3, :held] = jnp.max(mine, axis=0, keepdims=True)
 
 
-def pack(slots, offset, core, owner, ids, slot_of, active, counts, m_scale, v_scale, features, cotangent, chips):
-    blocks = features.shape[1] // LANES
-    rows = message_rows(slots, blocks)
-    return pl.pallas_call(
-        functools.partial(pack_kernel, slots, offset),
-        out_shape=(
-            jax.ShapeDtypeStruct((chips, rows // 4, 4, LANES), features.dtype),
-            jax.ShapeDtypeStruct((8, LANES), jnp.float32),
-        ),
-        in_specs=[SMEM, SMEM] + [VMEM] * 6 + [ANY, VMEM],
+def pack(slots, chips, core, owner, offset, small, cotangent, features):
+    rows = message_rows(slots, features.shape[1] // LANES)
+    like = jax.ShapeDtypeStruct
+    return pl.pallas_call(
+        functools.partial(pack_kernel, slots),
+        out_shape=(like((chips, rows // 4, 4, LANES), features.dtype), like((8, LANES), jnp.float32)),
+        in_specs=[SMEM] * 3 + [VMEM] * 7 + [ANY],
         out_specs=(VMEM, VMEM),
         scratch_shapes=[
             pltpu.VMEM((chips * rows, LANES), jnp.float32),
@@ -124,10 +121,10 @@
         ],
         compiler_params=GRANT,
         name=f"pack{slots}",
-    )(core, owner, ids, slot_of, active, counts, m_scale, v_scale, features, cotangent)
-
-
-def grad_kernel(slots, in_ref, own_ref, other_ref, flag_ref, scr):
+    )(core, owner, offset, *small, cotangent, features)
+
+
+def grad_kernel(slots, offset_ref, in_ref, own_ref, other_ref, next_ref, scr):
     chips, tiles = in_ref.shape[0], in_ref.shape[1]
     rows = tiles * 4
     half, columns = own_ref.shape
@@ -137,6 +134,8 @@
     scr[...] = in_ref[...].reshape(chips * rows, LANES).astype(f32)
     low = iota((chips, LANES), 1) < rank
     tags = scr[pl.ds(rows - 1, chips, stride=rows), :]
+    more = jnp.max(tags[:, 4 * slots : 4 * slots + 1]) > 0
+    next_ref[0] = jnp.where(more, offset_ref[0] + slots, 0)
     weights, wide = [], []
     for i in range(slots):
         pair = scr[pl.ds(slots * blocks + i // 2, chips, stride=rows), :]
@@ -160,28 +159,25 @@
         preferred_element_type=f32,
     )
     own_ref[...] = total[:half]
-    other_ref[:half, :] = total[half:]
-    more = jnp.max(tags[:, 4 * slots : 4 * slots + 1], axis=0, keepdims=True)
-    other_ref[half:, :] = jnp.broadcast_to(more, (8, columns))
-    flag_ref[...] = jnp.broadcast_to(more, flag_ref.shape)
-
-
-def partial_gradients(slots, received, half, columns):
+    other_ref[...] = total[half:]
+
+
+def partial_gradients(slots, offset, received, half, columns):
     chips, tiles = received.shape[0], received.shape[1]
     f32 = jnp.float32
     return pl.pallas_call(
         functools.partial(grad_kernel, slots),
         out_shape=(
             jax.ShapeDtypeStruct((half, columns), f32),
-            jax.ShapeDtypeStruct((half + 8, columns), f32),
-            jax.ShapeDtypeStruct((8, LANES), f32),
+            jax.ShapeDtypeStruct((half, columns), f32),
+            jax.ShapeDtypeStruct((1,), jnp.int32),
         ),
-        in_specs=[VMEM],
-        out_specs=(VMEM, VMEM, VMEM),
+        in_specs=[SMEM, VMEM],
+        out_specs=(VMEM, VMEM, SMEM),
         scratch_shapes=[pltpu.VMEM((chips * tiles * 4, LANES), f32)],
         compiler_params=GRANT,
         name=f"grad{slots}",
-    )(received)
+    )(offset, received)
 
 
 def moments(j, aux_ref, gradient, mc_ref, vc_ref, spread):
@@ -208,13 +204,9 @@
     return jnp.broadcast_to(aux_ref[2 * held + 2 : 2 * held + 3, j : j + 1], shape) > 0
 
 
-def serve_kernel(
-    aux_ref, own_ref, other_ref, flag_ref, weight_ref, mc_ref, vc_ref,
-    served_hbm, total_ref, more_ref, out_ref, sems,
-):
+def serve_kernel(aux_ref, own_ref, other_ref, weight_ref, mc_ref, vc_ref, served_hbm, total_ref, out_ref, sems):
     held, rank, columns = weight_ref.shape
     spread = row_spread(rank)
-    more_ref[...] = flag_ref[...] + other_ref[held * rank :, :LANES]
     sends = []
     for j in range(held):
         at = slice(j * rank, (j + 1) * rank)
@@ -233,29 +225,50 @@
         send.wait()
 
 
-def serve(replicas, aux, own, other, flag, weight, m_code, v_code):
+def serve(replicas, aux, own, other, weight, m_code, v_code):
     held = weight.shape[0]
     like = jax.ShapeDtypeStruct
     return pl.pallas_call(
         serve_kernel,
-        out_shape=(
-            like((replicas, *weight.shape), weight.dtype),
-            like(own.shape, jnp.float32),
-            like(flag.shape, jnp.float32),
-        ),
-        in_specs=[VMEM] * 7,
-        out_specs=(ANY, VMEM, VMEM),
+        out_shape=(like((replicas, *weight.shape), weight.dtype), like(own.shape, jnp.float32)),
+        in_specs=[VMEM] * 6,
+        out_specs=(ANY, VMEM),
         scratch_shapes=[
             pltpu.VMEM(weight.shape, weight.dtype),
             pltpu.SemaphoreType.DMA((held, replicas)),
         ],
         compiler_params=GRANT,
         name="serve",
-    )(aux, own, other, flag, weight, m_code, v_code)
+    )(aux, own, other, weight, m_code, v_code)
+
+
+def assemble_kernel(parts_ref, out_ref, sems):
+    replicas, columns = parts_ref.shape[0], parts_ref.shape[3]
+    moves = [
+        pltpu.make_async_copy(parts_ref.at[r], out_ref.at[:, :, pl.ds(r * columns, columns)], sems.at[r])
+        for r in range(replicas)
+    ]
+    for move in moves:
+        move.start()
+    for move in moves:
+        move.wait()
+
+
+def assemble(parts):
+    replicas, held, rank, columns = parts.shape
+    return pl.pallas_call(
+        assemble_kernel,
+        out_shape=jax.ShapeDtypeStruct((held, rank, replicas * columns), parts.dtype),
+        in_specs=[ANY],
+        out_specs=ANY,
+        scratch_shapes=[pltpu.SemaphoreType.DMA((replicas,))],
+        compiler_params=GRANT,
+        name="assemble",
+    )(parts)
 
 
 def state_kernel(
-    aux_ref, total_ref, flag_ref, mc_ref, vc_ref, dir_ref, mc_out, ms_out, vc_out, vs_out, more_ref
+    aux_ref, total_ref, mc_ref, vc_ref, dir_ref, mc_out, ms_out, vc_out, vs_out
 ):
     f32 = jnp.float32
     held, rank, columns = mc_ref.shape
@@ -268,7 +281,6 @@
     def per_row(scales):
         return jnp.sum(jnp.where(spread, scales, 0.0), axis=1, keepdims=True)
 
-    more_ref[...] = flag_ref[...]
     for j in range(held):
         gradient = total_ref[j * rank : (j + 1) * rank, :]
         moment, second, direction = moments(j, aux_ref, gradient, mc_ref, vc_ref, spread)
@@ -284,7 +296,7 @@
         vs_out[j : j + 1, :] = jnp.where(keep_row, v_new, aux_ref[held + j : held + j + 1, :pairs])
 
 
-def state(aux, total, flag, m_code, v_code):
+def state(aux, total, m_code, v_code):
     f32 = jnp.float32
     like = jax.ShapeDtypeStruct
     scales = like((m_code.shape[0], m_code.shape[1] // 2), f32)
@@ -296,13 +308,12 @@
             scales,
             like(v_code.shape, v_code.dtype),
             scales,
-            like(flag.shape, f32),
         ),
-        in_specs=[VMEM] * 5,
-        out_specs=(VMEM,) * 6,
+        in_specs=[VMEM] * 4,
+        out_specs=(VMEM,) * 5,
         compiler_params=GRANT,
         name="state",
-    )(aux, total, flag, m_code, v_code)
+    )(aux, total, m_code, v_code)
 
 
 def on_device(
@@ -316,34 +327,28 @@
     replicas = lax.axis_size("replica")
     core = lax.axis_index("core").astype(jnp.int32).reshape(1)
     owner = lax.axis_index(("x", "z", "core")).astype(jnp.int32).reshape(1)
-    arrays = (
+    small = (
         adapter_ids.reshape(1, -1), slot_of.reshape(1, -1), active_ids.reshape(1, -1), step_counts.reshape(1, -1),
-        m_scale.reshape(held, -1), v_scale.reshape(held, -1), features, cotangent.T,
-    )
-    swap = [(0, 1), (1, 0)]
-
-    def exchange(slots, offset, core):
-        sent, aux = pack(slots, offset, core, owner, *arrays, chips)
+        m_scale.reshape(held, -1), v_scale.reshape(held, -1),
+    )
+
+    def exchange(slots, offset):
+        sent, aux = pack(slots, chips, core, owner, offset, small, cotangent.T, features)
         received = lax.all_to_all(sent, ("x", "z"), split_axis=0, concat_axis=0, tiled=True)
-        own, other, flag = partial_gradients(slots, received, half, columns)
-        return own, lax.ppermute(other, "core", swap), flag, aux
-
-    def update(own, other, flag, aux):
-        copies, total, more = serve(replicas, aux, own, other, flag, weight, m_code, v_code)
-        parts = lax.all_to_all(copies, "replica", split_axis=0, concat_axis=0, tiled=True)
-        served = jnp.moveaxis(parts, 0, 2).reshape(held, rank, -1)
-        direction, m_new, ms_new, v_new, vs_new, more = state(aux, total, more, m_code, v_code)
-        return total, (more[0, 0], direction, m_new, ms_new, v_new, vs_new, served)
-
-    total, results = update(*exchange(FIRST, 0, core))
-
-    def with_the_rest(carry):
-        here = core + (carry[0] < 0).astype(jnp.int32)
-        own, other, flag, aux = exchange(8 - FIRST, FIRST, here)
-        return update(total + own, other, flag, aux)[1]
-
-    results = lax.while_loop(lambda carry: carry[0] > 0, with_the_rest, results)
-    _, direction, m_new, ms_new, v_new, vs_new, served = results
+        return partial_gradients(slots, offset, received, half, columns), aux
+
+    def another(carry):
+        own, other, rank_next = carry
+        (more_own, more_other, rank_next), _ = exchange(1, rank_next)
+        return own + more_own, other + more_other, rank_next
+
+    carry, aux = exchange(FIRST, jnp.zeros((1,), jnp.int32))
+    own, other, _ = lax.while_loop(lambda carry: carry[2][0] > 0, another, carry)
+    other = lax.ppermute(other, "core", [(0, 1), (1, 0)])
+    copies, total = serve(replicas, aux, own, other, weight, m_code, v_code)
+    parts = lax.all_to_all(copies, "replica", split_axis=0, concat_axis=0, tiled=True)
+    direction, m_new, ms_new, v_new, vs_new = state(aux, total, m_code, v_code)
+    served = assemble(parts)
     return (
         direction, m_new, ms_new.reshape(m_scale.shape), v_new, vs_new.reshape(v_scale.shape), served,
     )

time: 95.7 us -> 95.6 us (level)
  local copies, waits for them, and re-layouts: 2.51 us -> 0.84 us
  Pallas kernels: 5.76 us -> 6.73 us
    reshape x1 -> x0, local copies, waits for them, and re-layouts: 1.04 us -> none  [update(): served = jnp.moveaxis(parts, 0, 2).reshape(held, rank, -1)]
    pallas_call x1 -> x2, Pallas kernels: 1.72 us -> 2.68 us  [the longest x1 1.69 us: pack(): pl.pallas_call(functools.partial(pack_kernel, slots), out_shape=(like((ch...]
  transfers between devices with their start and end apart: 2 -> 2, of which waited for: 2 -> 2; matrix products, arithmetic and copies ran while one was open for 1% -> 0% of each run, Pallas kernels for 2% -> 2%
where the time goes in v1:
time: 95.6 us; the launch traced here: 95.2 us
  blocking collectives  64.2 us (67%)
  waiting for transfers between devices  15.6 us (16%)
  Pallas kernels  6.73 us (7%)
  starting transfers between devices  6.4 us (7%)
    all_to_all x1, blocking collectives, exchange(): lax.all_to_all(sent, ('x', 'z'), split_axis=0, concat_axis=0, tiled=True)  64.2 us
    all_to_all x1, waiting for transfers between devices, on_device(): lax.all_to_all(copies, 'replica', split_axis=0, concat_axis=0, tiled=True)  13.7 us
    all_to_all x1, starting transfers between devices, on_device(): lax.all_to_all(copies, 'replica', split_axis=0, concat_axis=0, tiled=True)  4.48 us
    ppermute x1, starting transfers between devices, on_device(): other = lax.ppermute(other, 'core', [(0, 1), (1, 0)])  1.92 us
  transfers between devices with their start and end apart: 2, of which 2 were waited for; matrix products, arithmetic and copies ran while one was open for 0% of the time, Pallas kernels for 2%

profile of v1, /device:TPU:6, one launch (start us, length us, event | category | flops | bytes accessed | tf_op | source)
XLA Modules:
  0.0 95.2 jit_solution(5403954004177633478)
XLA Ops:
  0.6 0.0 copy-start.4
  0.7 0.0 copy-start.8
  0.7 0.0 copy-start.9
  0.7 0.0 copy-start.6
  0.7 0.0 copy-start.7
  0.7 0.0 copy-start.5
  0.7 0.0 copy-start.10
  0.7 0.7 copy-done.4
  1.4 0.0 copy-done.8
  1.4 0.0 copy-done.5
  1.4 0.0 copy-done.10
  1.4 1.7 %pack6.1 = (bf16[64,13,4,128]{3,2,1,0:T(4,128)(2,1)S(1)}, f32[8,128]{1,0:T(8,128)S(1)}) custom-call(s32[1]{0:T(128)} %bitcast.2.core_ref, s32[1]{0:T(128)} %bitcast.3.owner_ref, s32[1]{0:T(128)} %constant.24.clone.1.offset_ref, s32[1,256]{1,0:T(1,128)S(1)} %bitcast.19, s32[1,256]{1,0:T(1,128)S(1)} %bitcast.21, s32[1,192]{1,0:T(1,128)S(1)} %bitcast.23, ...), custom_call_target="tpu_custom_call" | custom-call | tf_op jit(solution)/shard_map/pack6/pallas_call | solution.py:112
  3.1 64.2 %all_to_all.15.in_ref = bf16[64,13,4,128]{3,2,1,0:T(4,128)(2,1)S(1)} all-to-all(bf16[64,13,4,128]{3,2,1,0:T(4,128)(2,1)S(1)} %get-tuple-element.91), channel_id=1, replica_groups=mesh['x'=4,'z'=16,'core'=2,'replica'=4] {'x','z'}, dimensions={0} | all-to-all | bytes 1703936 | tf_op jit(solution)/shard_map/all_to_all | solution.py:337
  67.3 0.9 grad6.1
  68.2 0.1 copy-done.3
  68.3 0.7 while.11
  69.1 1.9 %collective-permute-start = (f32[128,1024]{1,0:T(8,128)S(1)}, f32[128,1024]{1,0:T(8,128)S(1)}, u32[]{:S(2)}, u32[]{:S(2)}) collective-permute-start(f32[128,1024]{1,0:T(8,128)S(1)} %get-tuple-element.96), channel_id=1, source_target_pairs={{0,4},{4,0},{1,5},{5,1},{2,6},{6,2},{3,7},{7,3},{8,12},{12,8},{9,1... | collective-permute-start | bytes 1572872 | tf_op jit(solution)/shard_map/ppermute | solution.py:347
  71.0 1.9 %collective-permute-done.other_ref = f32[128,1024]{1,0:T(8,128)S(1)} collective-permute-done((f32[128,1024]{1,0:T(8,128)S(1)}, f32[128,1024]{1,0:T(8,128)S(1)}, u32[]{:S(2)}, u32[]{:S(2)}) %collective-permute-start) | collective-permute-done | bytes 524320 | tf_op jit(solution)/shard_map/ppermute | solution.py:347
  72.9 0.0 copy-done.1
  72.9 1.5 %serve.1 = (bf16[4,2,64,1024]{3,2,1,0:T(8,128)(2,1)}, f32[128,1024]{1,0:T(8,128)S(1)}) custom-call(f32[8,128]{1,0:T(8,128)S(1)} %get-tuple-element.90.aux_ref, f32[128,1024]{1,0:T(8,128)S(1)} %get-tuple-element.95.own_ref, f32[128,1024]{1,0:T(8,128)S(1)} %collective-permute-done.other_ref, bf16[2,64,1024]{2,1,0:T(8,128)(2,1)S(1)} %copy-done.2, ...), custom_call_target="tpu_custom_call" | custom-call | tf_op jit(solution)/shard_map/serve/pallas_call | solution.py:231
  74.3 4.5 %all-to-all-start.2 = ((bf16[4,2,64,1024]{3,2,1,0:T(8,128)(2,1)}), bf16[4,2,64,1024]{3,2,1,0:T(8,128)(2,1)S(1)}, u32[]{:S(2)}, u32[]{:S(2)}) async-start(bf16[4,2,64,1024]{3,2,1,0:T(8,128)(2,1)} %get-tuple-element.103), calls=%async_computation.2 | async-start | bytes 2097152 | tf_op jit(solution)/shard_map/all_to_all | solution.py:349
  78.8 1.7 %state.1 = (f32[2,64,1024]{2,1,0:T(8,128)}, bf16[2,64,1024]{2,1,0:T(8,128)(2,1)}, f32[2,32]{1,0:T(2,128)}, bf16[2,64,1024]{2,1,0:T(8,128)(2,1)}, f32[2,32]{1,0:T(2,128)}) custom-call(f32[8,128]{1,0:T(8,128)S(1)} %get-tuple-element.90.aux_ref, f32[128,1024]{1,0:T(8,128)S(1)} %get-tuple-element.97.total_ref, bf16[2,64,1024]{2,1,0:T(8,128)(2,1)S(1)} %copy-done, ...), custom_call_target="tpu_custom_call" | custom-call | tf_op jit(solution)/shard_map/state/pallas_call | solution.py:303
  80.5 13.7 %all-to-all-done.2.parts_ref = bf16[4,2,64,1024]{3,2,1,0:T(8,128)(2,1)S(1)} async-done(((bf16[4,2,64,1024]{3,2,1,0:T(8,128)(2,1)}), bf16[4,2,64,1024]{3,2,1,0:T(8,128)(2,1)S(1)}, u32[]{:S(2)}, u32[]{:S(2)}) %all-to-all-start.2) | async-done | bytes 1048608 | tf_op jit(solution)/shard_map/all_to_all | solution.py:349
  94.2 1.0 %assemble.1 = bf16[2,64,4096]{2,1,0:T(8,128)(2,1)} custom-call(bf16[4,2,64,1024]{3,2,1,0:T(8,128)(2,1)S(1)} %all-to-all-done.2.parts_ref), custom_call_target="tpu_custom_call" | custom-call | tf_op jit(solution)/shard_map/assemble/pallas_call | solution.py:259
  (9 shorter events, 0.0 us)
Async XLA Ops:
  0.6 0.8 copy-start.4
  0.7 0.7 copy-start.8
  0.7 0.7 copy-start.9
  0.7 0.7 copy-start.6
  0.7 0.7 copy-start.7
  0.7 0.7 copy-start.5
  0.7 0.7 copy-start.10
  67.3 1.0 %copy-start.3 = (bf16[256,1024]{1,0:T(8,128)(2,1)S(1)}, bf16[256,1024]{1,0:T(8,128)(2,1)}, u32[]{:S(2)}) copy-start(bf16[256,1024]{1,0:T(8,128)(2,1)} %feat_hbm.1) | copy-start | bytes 1572868
  68.3 4.5 %copy-start = (bf16[2,64,1024]{2,1,0:T(8,128)(2,1)S(1)}, bf16[2,64,1024]{2,1,0:T(8,128)(2,1)}, u32[]{:S(2)}) copy-start(bf16[2,64,1024]{2,1,0:T(8,128)(2,1)} %mc_ref.3) | copy-start | bytes 786436
  68.3 4.5 %copy-start.1 = (bf16[2,64,1024]{2,1,0:T(8,128)(2,1)S(1)}, bf16[2,64,1024]{2,1,0:T(8,128)(2,1)}, u32[]{:S(2)}) copy-start(bf16[2,64,1024]{2,1,0:T(8,128)(2,1)} %vc_ref.3) | copy-start | bytes 786436
  68.3 4.5 %copy-start.2 = (bf16[2,64,1024]{2,1,0:T(8,128)(2,1)S(1)}, bf16[2,64,1024]{2,1,0:T(8,128)(2,1)}, u32[]{:S(2)}) copy-start(bf16[2,64,1024]{2,1,0:T(8,128)(2,1)} %weight_ref.1) | copy-start | bytes 786436
  69.1 3.8 %collective-permute-start = (f32[128,1024]{1,0:T(8,128)S(1)}, f32[128,1024]{1,0:T(8,128)S(1)}, u32[]{:S(2)}, u32[]{:S(2)}) collective-permute-start(f32[128,1024]{1,0:T(8,128)S(1)} %get-tuple-element.96), channel_id=1, source_target_pairs={{0,4},{4,0},{1,5},{5,1},{2,6},{6,2},{3,7},{7,3},{8,12},{12,8},{9,1... | collective-permute-start | bytes 1572872 | tf_op jit(solution)/shard_map/ppermute | solution.py:347
  74.3 19.9 %all-to-all-start.2 = ((bf16[4,2,64,1024]{3,2,1,0:T(8,128)(2,1)}), bf16[4,2,64,1024]{3,2,1,0:T(8,128)(2,1)S(1)}, u32[]{:S(2)}, u32[]{:S(2)}) async-start(bf16[4,2,64,1024]{3,2,1,0:T(8,128)(2,1)} %get-tuple-element.103), calls=%async_computation.2 | async-start | bytes 2097152 | tf_op jit(solution)/shard_map/all_to_all | solution.py:349

commit v2 on v1

--- a/solution.py
+++ b/solution.py
@@ -16,6 +16,7 @@
 decay_rate = 0.01
 
 LANES = 128
+PIECES = 2
 FIRST = 6
 VMEM = pl.BlockSpec(memory_space=pltpu.VMEM)
 SMEM = pl.BlockSpec(memory_space=pltpu.SMEM)
@@ -72,12 +73,7 @@
         preferred_element_type=f32,
     )
     beside = dot(chosen, beside.astype(bf16))
-    fetch.wait()
-    moved = dot(chosen, feat_ref[...])
     of_slot = [slice(i * chips, (i + 1) * chips) for i in range(slots)]
-    for i in range(slots):
-        for b in range(blocks):
-            scr[pl.ds(i * blocks + b, chips, stride=rows), :] = moved[of_slot[i], b * LANES : (b + 1) * LANES]
     lane = iota((chips, LANES), 1)
     tags = jnp.where(lane == 4 * slots, more, 0.0)
     for i in range(slots):
@@ -90,7 +86,6 @@
         scr[pl.ds(slots * blocks + p, chips, stride=rows), :] = pair
     for r in range(slots * blocks + (slots + 1) // 2, rows):
         scr[pl.ds(r, chips, stride=rows), :] = tags
-    out_ref[...] = scr[...].astype(out_ref.dtype).reshape(chips, tiles, 4, LANES)
 
     aux_ref[...] = jnp.zeros(aux_ref.shape, f32)
     aux_ref[:held, :pairs] = ms_ref[...]
@@ -104,6 +99,13 @@
     state_row = iota((state_rows, held), 0) - held * owner
     mine = jnp.where(state_row == iota((state_rows, held), 1), trained, 0.0)
     aux_ref[2 * held + 2 : 2 * held + 3, :held] = jnp.max(mine, axis=0, keepdims=True)
+
+    fetch.wait()
+    moved = dot(chosen, feat_ref[...])
+    for i in range(slots):
+        for b in range(blocks):
+            scr[pl.ds(i * blocks + b, chips, stride=rows), :] = moved[of_slot[i], b * LANES : (b + 1) * LANES]
+    out_ref[...] = scr[...].astype(out_ref.dtype).reshape(chips, tiles, 4, LANES)
 
 
 def pack(slots, chips, core, owner, offset, small, cotangent, features):
@@ -180,7 +182,7 @@
     )(offset, received)
 
 
-def moments(j, aux_ref, gradient, mc_ref, vc_ref, spread):
+def moments(j, aux_ref, gradient, mc_ref, vc_ref, spread, at=slice(None)):
     f32 = jnp.float32
     held, rank, _ = mc_ref.shape
     pairs = rank // 2
@@ -188,8 +190,8 @@
     def per_row(at):
         return jnp.sum(jnp.where(spread, aux_ref[at : at + 1, :pairs], 0.0), axis=1, keepdims=True)
 
-    moment = mc_ref[j].astype(f32) * (beta_one * per_row(j)) + (1.0 - beta_one) * gradient
-    second = vc_ref[j].astype(f32) * (beta_two * per_row(held + j)) + (1.0 - beta_two) * gradient * gradient
+    moment = mc_ref[j, :, at].astype(f32) * (beta_one * per_row(j)) + (1.0 - beta_one) * gradient
+    second = vc_ref[j, :, at].astype(f32) * (beta_two * per_row(held + j)) + (1.0 - beta_two) * gradient * gradient
     inverse_one = aux_ref[2 * held : 2 * held + 1, j : j + 1]
     inverse_two = aux_ref[2 * held + 1 : 2 * held + 2, j : j + 1]
     direction = (moment * inverse_one) / (jnp.sqrt(second * inverse_two) + adam_eps)
@@ -207,18 +209,21 @@
 def serve_kernel(aux_ref, own_ref, other_ref, weight_ref, mc_ref, vc_ref, served_hbm, total_ref, out_ref, sems):
     held, rank, columns = weight_ref.shape
     spread = row_spread(rank)
+    width = columns // PIECES
     sends = []
-    for j in range(held):
-        at = slice(j * rank, (j + 1) * rank)
-        gradient = own_ref[at, :] + other_ref[at, :]
-        total_ref[at, :] = gradient
-        _, _, direction = moments(j, aux_ref, gradient, mc_ref, vc_ref, spread)
-        weight = weight_ref[j].astype(jnp.float32)
+    for n in range(held * PIECES):
+        j, first = n // PIECES, n % PIECES * width
+        rows, at = slice(j * rank, (j + 1) * rank), slice(first, first + width)
+        gradient = own_ref[rows, at] + other_ref[rows, at]
+        total_ref[rows, at] = gradient
+        _, _, direction = moments(j, aux_ref, gradient, mc_ref, vc_ref, spread, at)
+        weight = weight_ref[j, :, at].astype(jnp.float32)
         served = weight - learn_rate * (direction + decay_rate * weight)
         served = jnp.where(trained_row(aux_ref, held, j, weight.shape), served, weight)
-        out_ref[j] = served.astype(out_ref.dtype)
+        out_ref[j, :, at] = served.astype(out_ref.dtype)
+        piece = (slice(None), pl.ds(first, width))
         for r in range(served_hbm.shape[0]):
-            send = pltpu.make_async_copy(out_ref.at[j], served_hbm.at[r, j], sems.at[j, r])
+            send = pltpu.make_async_copy(out_ref.at[j, *piece], served_hbm.at[r, j, *piece], sems.at[n, r])
             send.start()
             sends.append(send)
     for send in sends:
@@ -235,7 +240,7 @@
         out_specs=(ANY, VMEM),
         scratch_shapes=[
             pltpu.VMEM(weight.shape, weight.dtype),
-            pltpu.SemaphoreType.DMA((held, replicas)),
+            pltpu.SemaphoreType.DMA((held * PIECES, replicas)),
         ],
         compiler_params=GRANT,
         name="serve",

time: 95.6 us -> 95.5 us (level)
  no operation moved by 1% of the time
where the time goes in v2:
time: 95.5 us; the launch traced here: 95.1 us
  blocking collectives  64.2 us (67%)
  waiting for transfers between devices  15.6 us (16%)
  Pallas kernels  6.67 us (7%)
  starting transfers between devices  6.4 us (7%)
    all_to_all x1, blocking collectives, exchange(): lax.all_to_all(sent, ('x', 'z'), split_axis=0, concat_axis=0, tiled=True)  64.2 us
    all_to_all x1, waiting for transfers between devices, on_device(): lax.all_to_all(copies, 'replica', split_axis=0, concat_axis=0, tiled=True)  13.7 us
    all_to_all x1, starting transfers between devices, on_device(): lax.all_to_all(copies, 'replica', split_axis=0, concat_axis=0, tiled=True)  4.48 us
    ppermute x1, starting transfers between devices, on_device(): other = lax.ppermute(other, 'core', [(0, 1), (1, 0)])  1.92 us
  transfers between devices with their start and end apart: 2, of which 2 were waited for; matrix products, arithmetic and copies ran while one was open for 0% of the time, Pallas kernels for 2%

profile of v2, /device:TPU:6, one launch (start us, length us, event | category | flops | bytes accessed | tf_op | source)
XLA Modules:
  0.0 95.1 jit_solution(2387104699420000680)
XLA Ops:
  0.6 0.0 copy-start.4
  0.7 0.0 copy-start.8
  0.7 0.0 copy-start.9
  0.7 0.0 copy-start.6
  0.7 0.0 copy-start.7
  0.7 0.0 copy-start.5
  0.7 0.0 copy-start.10
  0.7 0.7 copy-done.4
  1.4 0.0 copy-done.8
  1.4 0.0 copy-done.5
  1.4 0.0 copy-done.10
  1.4 1.6 %pack6.1 = (bf16[64,13,4,128]{3,2,1,0:T(4,128)(2,1)S(1)}, f32[8,128]{1,0:T(8,128)S(1)}) custom-call(s32[1]{0:T(128)} %bitcast.2.core_ref, s32[1]{0:T(128)} %bitcast.3.owner_ref, s32[1]{0:T(128)} %constant.24.clone.1.offset_ref, s32[1,256]{1,0:T(1,128)S(1)} %bitcast.19, s32[1,256]{1,0:T(1,128)S(1)} %bitcast.21, s32[1,192]{1,0:T(1,128)S(1)} %bitcast.23, ...), custom_call_target="tpu_custom_call" | custom-call | tf_op jit(solution)/shard_map/pack6/pallas_call | solution.py:114
  3.1 64.2 %all_to_all.15.in_ref = bf16[64,13,4,128]{3,2,1,0:T(4,128)(2,1)S(1)} all-to-all(bf16[64,13,4,128]{3,2,1,0:T(4,128)(2,1)S(1)} %get-tuple-element.91), channel_id=1, replica_groups=mesh['x'=4,'z'=16,'core'=2,'replica'=4] {'x','z'}, dimensions={0} | all-to-all | bytes 1703936 | tf_op jit(solution)/shard_map/all_to_all | solution.py:342
  67.2 0.9 grad6.1
  68.1 0.1 copy-done.3
  68.3 0.7 while.11
  69.0 1.9 %collective-permute-start = (f32[128,1024]{1,0:T(8,128)S(1)}, f32[128,1024]{1,0:T(8,128)S(1)}, u32[]{:S(2)}, u32[]{:S(2)}) collective-permute-start(f32[128,1024]{1,0:T(8,128)S(1)} %get-tuple-element.96), channel_id=1, source_target_pairs={{0,4},{4,0},{1,5},{5,1},{2,6},{6,2},{3,7},{7,3},{8,12},{12,8},{9,1... | collective-permute-start | bytes 1572872 | tf_op jit(solution)/shard_map/ppermute | solution.py:352
  70.9 1.9 %collective-permute-done.other_ref = f32[128,1024]{1,0:T(8,128)S(1)} collective-permute-done((f32[128,1024]{1,0:T(8,128)S(1)}, f32[128,1024]{1,0:T(8,128)S(1)}, u32[]{:S(2)}, u32[]{:S(2)}) %collective-permute-start) | collective-permute-done | bytes 524320 | tf_op jit(solution)/shard_map/ppermute | solution.py:352
  72.8 0.0 copy-done
  72.8 1.5 %serve.1 = (bf16[4,2,64,1024]{3,2,1,0:T(8,128)(2,1)}, f32[128,1024]{1,0:T(8,128)S(1)}) custom-call(f32[8,128]{1,0:T(8,128)S(1)} %get-tuple-element.90.aux_ref, f32[128,1024]{1,0:T(8,128)S(1)} %get-tuple-element.95.own_ref, f32[128,1024]{1,0:T(8,128)S(1)} %collective-permute-done.other_ref, bf16[2,64,1024]{2,1,0:T(8,128)(2,1)S(1)} %copy-done.2, ...), custom_call_target="tpu_custom_call" | custom-call | tf_op jit(solution)/shard_map/serve/pallas_call | solution.py:236
  74.3 4.5 %all-to-all-start.2 = ((bf16[4,2,64,1024]{3,2,1,0:T(8,128)(2,1)}), bf16[4,2,64,1024]{3,2,1,0:T(8,128)(2,1)S(1)}, u32[]{:S(2)}, u32[]{:S(2)}) async-start(bf16[4,2,64,1024]{3,2,1,0:T(8,128)(2,1)} %get-tuple-element.103), calls=%async_computation.2 | async-start | bytes 2097152 | tf_op jit(solution)/shard_map/all_to_all | solution.py:354
  78.8 1.7 %state.1 = (f32[2,64,1024]{2,1,0:T(8,128)}, bf16[2,64,1024]{2,1,0:T(8,128)(2,1)}, f32[2,32]{1,0:T(2,128)}, bf16[2,64,1024]{2,1,0:T(8,128)(2,1)}, f32[2,32]{1,0:T(2,128)}) custom-call(f32[8,128]{1,0:T(8,128)S(1)} %get-tuple-element.90.aux_ref, f32[128,1024]{1,0:T(8,128)S(1)} %get-tuple-element.97.total_ref, bf16[2,64,1024]{2,1,0:T(8,128)(2,1)S(1)} %copy-done, ...), custom_call_target="tpu_custom_call" | custom-call | tf_op jit(solution)/shard_map/state/pallas_call | solution.py:308
  80.4 13.7 %all-to-all-done.2.parts_ref = bf16[4,2,64,1024]{3,2,1,0:T(8,128)(2,1)S(1)} async-done(((bf16[4,2,64,1024]{3,2,1,0:T(8,128)(2,1)}), bf16[4,2,64,1024]{3,2,1,0:T(8,128)(2,1)S(1)}, u32[]{:S(2)}, u32[]{:S(2)}) %all-to-all-start.2) | async-done | bytes 1048608 | tf_op jit(solution)/shard_map/all_to_all | solution.py:354
  94.1 1.0 %assemble.1 = bf16[2,64,4096]{2,1,0:T(8,128)(2,1)} custom-call(bf16[4,2,64,1024]{3,2,1,0:T(8,128)(2,1)S(1)} %all-to-all-done.2.parts_ref), custom_call_target="tpu_custom_call" | custom-call | tf_op jit(solution)/shard_map/assemble/pallas_call | solution.py:264
  (9 shorter events, 0.0 us)
Async XLA Ops:
  0.6 0.8 copy-start.4
  0.7 0.7 copy-start.8
  0.7 0.7 copy-start.9
  0.7 0.7 copy-start.6
  0.7 0.7 copy-start.7
  0.7 0.7 copy-start.5
  0.7 0.7 copy-start.10
  67.2 1.0 %copy-start.3 = (bf16[256,1024]{1,0:T(8,128)(2,1)S(1)}, bf16[256,1024]{1,0:T(8,128)(2,1)}, u32[]{:S(2)}) copy-start(bf16[256,1024]{1,0:T(8,128)(2,1)} %feat_hbm.1) | copy-start | bytes 1572868
  68.3 4.5 %copy-start = (bf16[2,64,1024]{2,1,0:T(8,128)(2,1)S(1)}, bf16[2,64,1024]{2,1,0:T(8,128)(2,1)}, u32[]{:S(2)}) copy-start(bf16[2,64,1024]{2,1,0:T(8,128)(2,1)} %mc_ref.3) | copy-start | bytes 786436
  68.3 4.5 %copy-start.1 = (bf16[2,64,1024]{2,1,0:T(8,128)(2,1)S(1)}, bf16[2,64,1024]{2,1,0:T(8,128)(2,1)}, u32[]{:S(2)}) copy-start(bf16[2,64,1024]{2,1,0:T(8,128)(2,1)} %vc_ref.3) | copy-start | bytes 786436
  68.3 4.5 %copy-start.2 = (bf16[2,64,1024]{2,1,0:T(8,128)(2,1)S(1)}, bf16[2,64,1024]{2,1,0:T(8,128)(2,1)}, u32[]{:S(2)}) copy-start(bf16[2,64,1024]{2,1,0:T(8,128)(2,1)} %weight_ref.1) | copy-start | bytes 786436
  69.0 3.8 %collective-permute-start = (f32[128,1024]{1,0:T(8,128)S(1)}, f32[128,1024]{1,0:T(8,128)S(1)}, u32[]{:S(2)}, u32[]{:S(2)}) collective-permute-start(f32[128,1024]{1,0:T(8,128)S(1)} %get-tuple-element.96), channel_id=1, source_target_pairs={{0,4},{4,0},{1,5},{5,1},{2,6},{6,2},{3,7},{7,3},{8,12},{12,8},{9,1... | collective-permute-start | bytes 1572872 | tf_op jit(solution)/shard_map/ppermute | solution.py:352
  74.3 19.9 %all-to-all-start.2 = ((bf16[4,2,64,1024]{3,2,1,0:T(8,128)(2,1)}), bf16[4,2,64,1024]{3,2,1,0:T(8,128)(2,1)S(1)}, u32[]{:S(2)}, u32[]{:S(2)}) async-start(bf16[4,2,64,1024]{3,2,1,0:T(8,128)(2,1)} %get-tuple-element.103), calls=%async_computation.2 | async-start | bytes 2097152 | tf_op jit(solution)/shard_map/all_to_all | solution.py:354

commit v3 on v2

--- a/solution.py
+++ b/solution.py
@@ -33,12 +33,26 @@
     return lax.broadcasted_iota(jnp.int32, shape, dim)
 
 
+def near_kernel(*refs):
+    del refs
+
+
+def near(*arrays):
+    return pl.pallas_call(
+        near_kernel,
+        out_shape=tuple(jax.ShapeDtypeStruct(a.shape, a.dtype) for a in arrays),
+        in_specs=[ANY] * len(arrays),
+        out_specs=(ANY,) * len(arrays),
+        input_output_aliases={n: n for n in range(len(arrays))},
+        compiler_params=GRANT,
+        name="near",
+    )(*arrays)
+
+
 def pack_kernel(
-    slots, core_ref, owner_ref, offset_ref, ids_ref, slot_ref, act_ref, count_ref, ms_ref, vs_ref, cot_ref, feat_hbm,
-    out_ref, aux_ref, scr, feat_ref, feat_sem,
+    slots, core_ref, owner_ref, offset_ref, ids_ref, slot_ref, act_ref, count_ref, ms_ref, vs_ref, cot_ref, feat_ref,
+    out_ref, aux_ref, scr,
 ):
-    fetch = pltpu.make_async_copy(feat_hbm, feat_ref, feat_sem)
-    fetch.start()
     rank, tokens = cot_ref.shape
     state_rows = slot_ref.shape[1]
     columns = feat_ref.shape[1]
@@ -100,7 +114,6 @@
     mine = jnp.where(state_row == iota((state_rows, held), 1), trained, 0.0)
     aux_ref[2 * held + 2 : 2 * held + 3, :held] = jnp.max(mine, axis=0, keepdims=True)
 
-    fetch.wait()
     moved = dot(chosen, feat_ref[...])
     for i in range(slots):
         for b in range(blocks):
@@ -114,13 +127,9 @@
     return pl.pallas_call(
         functools.partial(pack_kernel, slots),
         out_shape=(like((chips, rows // 4, 4, LANES), features.dtype), like((8, LANES), jnp.float32)),
-        in_specs=[SMEM] * 3 + [VMEM] * 7 + [ANY],
+        in_specs=[SMEM] * 3 + [VMEM] * 8,
         out_specs=(VMEM, VMEM),
-        scratch_shapes=[
-            pltpu.VMEM((chips * rows, LANES), jnp.float32),
-            pltpu.VMEM(features.shape, features.dtype),
-            pltpu.SemaphoreType.DMA,
-        ],
+        scratch_shapes=[pltpu.VMEM((chips * rows, LANES), jnp.float32)],
         compiler_params=GRANT,
         name=f"pack{slots}",
     )(core, owner, offset, *small, cotangent, features)
@@ -337,8 +346,10 @@
         m_scale.reshape(held, -1), v_scale.reshape(held, -1),
     )
 
+    *small, cot, close = near(*small, cotangent.T, features)
+
     def exchange(slots, offset):
-        sent, aux = pack(slots, chips, core, owner, offset, small, cotangent.T, features)
+        sent, aux = pack(slots, chips, core, owner, offset, small, cot, close)
         received = lax.all_to_all(sent, ("x", "z"), split_axis=0, concat_axis=0, tiled=True)
         return partial_gradients(slots, offset, received, half, columns), aux
 

time: 95.5 us -> 95.2 us (level)
  no operation moved by 1% of the time
where the time goes in v3:
time: 95.2 us; the launch traced here: 94.9 us
  blocking collectives  64.2 us (67%)
  waiting for transfers between devices  15.6 us (16%)
  starting transfers between devices  6.41 us (7%)
  Pallas kernels  6.19 us (7%)
  local copies, waits for them, and re-layouts  1 us (1%)
    all_to_all x1, blocking collectives, exchange(): lax.all_to_all(sent, ('x', 'z'), split_axis=0, concat_axis=0, tiled=True)  64.2 us
    all_to_all x1, waiting for transfers between devices, on_device(): lax.all_to_all(copies, 'replica', split_axis=0, concat_axis=0, tiled=True)  13.7 us
    all_to_all x1, starting transfers between devices, on_device(): lax.all_to_all(copies, 'replica', split_axis=0, concat_axis=0, tiled=True)  4.49 us
    ppermute x1, starting transfers between devices, on_device(): other = lax.ppermute(other, 'core', [(0, 1), (1, 0)])  1.92 us
  transfers between devices with their start and end apart: 2, of which 2 were waited for; matrix products, arithmetic and copies ran while one was open for 0% of the time, Pallas kernels for 2%

profile of v3, /device:TPU:6, one launch (start us, length us, event | category | flops | bytes accessed | tf_op | source)
XLA Modules:
  0.0 94.9 jit_solution(6678940922722408268)
XLA Ops:
  0.6 0.0 copy-start.3
  0.6 0.0 copy-start.4
  0.7 0.0 copy-start.6
  0.7 0.0 copy-start.7
  0.7 0.0 copy-start.8
  0.7 0.0 copy-start.9
  0.7 1.0 %copy-done.3 = bf16[256,1024]{1,0:T(8,128)(2,1)S(1)} copy-done((bf16[256,1024]{1,0:T(8,128)(2,1)S(1)}, bf16[256,1024]{1,0:T(8,128)(2,1)}, u32[]{:S(2)}) %copy-start.3) | copy-done | bytes 524312
  1.7 0.0 copy-done.6
  1.7 0.0 copy-done.8
  1.7 1.2 %pack6.1 = (bf16[64,13,4,128]{3,2,1,0:T(4,128)(2,1)S(1)}, f32[8,128]{1,0:T(8,128)S(1)}) custom-call(s32[1]{0:T(128)} %bitcast.1.core_ref, s32[1]{0:T(128)} %bitcast.2.owner_ref, s32[1]{0:T(128)} %constant.24.clone.1.offset_ref, s32[1,256]{1,0:T(1,128)S(1)} %get-tuple-element.170.ids_ref, s32[1,256]{1,0:T(1,128)S(1)} %get-tuple-element.171.slot_ref, ...), custom_call_target="tpu_custom_call" | custom-call | tf_op jit(solution)/shard_map/pack6/pallas_call | solution.py:127
  2.9 64.2 %all_to_all.15.in_ref = bf16[64,13,4,128]{3,2,1,0:T(4,128)(2,1)S(1)} all-to-all(bf16[64,13,4,128]{3,2,1,0:T(4,128)(2,1)S(1)} %get-tuple-element.107), channel_id=1, replica_groups=mesh['x'=4,'z'=16,'core'=2,'replica'=4] {'x','z'}, dimensions={0} | all-to-all | bytes 1703936 | tf_op jit(solution)/shard_map/all_to_all | solution.py:353
  67.1 0.9 grad6.1
  68.0 0.0 copy-start
  68.0 0.0 copy-start.1
  68.0 0.0 copy-start.2
  68.0 0.7 while.11
  68.7 1.9 %collective-permute-start = (f32[128,1024]{1,0:T(8,128)S(1)}, f32[128,1024]{1,0:T(8,128)S(1)}, u32[]{:S(2)}, u32[]{:S(2)}) collective-permute-start(f32[128,1024]{1,0:T(8,128)S(1)} %get-tuple-element.112), channel_id=1, source_target_pairs={{0,4},{4,0},{1,5},{5,1},{2,6},{6,2},{3,7},{7,3},{8,12},{12,8},{9,1... | collective-permute-start | bytes 1572872 | tf_op jit(solution)/shard_map/ppermute | solution.py:363
  70.7 1.9 %collective-permute-done.other_ref = f32[128,1024]{1,0:T(8,128)S(1)} collective-permute-done((f32[128,1024]{1,0:T(8,128)S(1)}, f32[128,1024]{1,0:T(8,128)S(1)}, u32[]{:S(2)}, u32[]{:S(2)}) %collective-permute-start) | collective-permute-done | bytes 524320 | tf_op jit(solution)/shard_map/ppermute | solution.py:363
  72.5 0.0 copy-done.1
  72.6 1.5 %serve.1 = (bf16[4,2,64,1024]{3,2,1,0:T(8,128)(2,1)}, f32[128,1024]{1,0:T(8,128)S(1)}) custom-call(f32[8,128]{1,0:T(8,128)S(1)} %get-tuple-element.106.aux_ref, f32[128,1024]{1,0:T(8,128)S(1)} %get-tuple-element.111.own_ref, f32[128,1024]{1,0:T(8,128)S(1)} %collective-permute-done.other_ref, bf16[2,64,1024]{2,1,0:T(8,128)(2,1)S(1)} %copy-done.2, ...), custom_call_target="tpu_custom_call" | custom-call | tf_op jit(solution)/shard_map/serve/pallas_call | solution.py:245
  74.0 4.5 %all-to-all-start.2 = ((bf16[4,2,64,1024]{3,2,1,0:T(8,128)(2,1)}), bf16[4,2,64,1024]{3,2,1,0:T(8,128)(2,1)S(1)}, u32[]{:S(2)}, u32[]{:S(2)}) async-start(bf16[4,2,64,1024]{3,2,1,0:T(8,128)(2,1)} %get-tuple-element.119), calls=%async_computation.2 | async-start | bytes 2097152 | tf_op jit(solution)/shard_map/all_to_all | solution.py:365
  78.5 1.7 %state.1 = (f32[2,64,1024]{2,1,0:T(8,128)}, bf16[2,64,1024]{2,1,0:T(8,128)(2,1)}, f32[2,32]{1,0:T(2,128)}, bf16[2,64,1024]{2,1,0:T(8,128)(2,1)}, f32[2,32]{1,0:T(2,128)}) custom-call(f32[8,128]{1,0:T(8,128)S(1)} %get-tuple-element.106.aux_ref, f32[128,1024]{1,0:T(8,128)S(1)} %get-tuple-element.113.total_ref, bf16[2,64,1024]{2,1,0:T(8,128)(2,1)S(1)} %copy-done, ...), custom_call_target="tpu_custom_call" | custom-call | tf_op jit(solution)/shard_map/state/pallas_call | solution.py:317
  80.2 13.7 %all-to-all-done.2.parts_ref = bf16[4,2,64,1024]{3,2,1,0:T(8,128)(2,1)S(1)} async-done(((bf16[4,2,64,1024]{3,2,1,0:T(8,128)(2,1)}), bf16[4,2,64,1024]{3,2,1,0:T(8,128)(2,1)S(1)}, u32[]{:S(2)}, u32[]{:S(2)}) %all-to-all-start.2) | async-done | bytes 1048608 | tf_op jit(solution)/shard_map/all_to_all | solution.py:365
  93.9 1.0 %assemble.1 = bf16[2,64,4096]{2,1,0:T(8,128)(2,1)} custom-call(bf16[4,2,64,1024]{3,2,1,0:T(8,128)(2,1)S(1)} %all-to-all-done.2.parts_ref), custom_call_target="tpu_custom_call" | custom-call | tf_op jit(solution)/shard_map/assemble/pallas_call | solution.py:273
  (10 shorter events, 0.0 us)
Async XLA Ops:
  0.6 1.0 %copy-start.3 = (bf16[256,1024]{1,0:T(8,128)(2,1)S(1)}, bf16[256,1024]{1,0:T(8,128)(2,1)}, u32[]{:S(2)}) copy-start(bf16[256,1024]{1,0:T(8,128)(2,1)} %param.13) | copy-start | bytes 1572868
  0.6 1.0 %copy-start.4 = (bf16[256,64]{0,1:T(8,128)(2,1)S(1)}, bf16[256,64]{0,1:T(8,128)(2,1)}, u32[]{:S(2)}) copy-start(bf16[256,64]{0,1:T(8,128)(2,1)} %param.14) | copy-start | bytes 98308
  0.7 1.0 %copy-start.6 = (s32[256]{0:T(256)S(1)}, s32[256]{0:T(256)}, u32[]{:S(2)}) copy-start(s32[256]{0:T(256)} %param.16) | copy-start | bytes 3076
  0.7 1.0 %copy-start.7 = (s32[192]{0:T(256)S(1)}, s32[192]{0:T(256)}, u32[]{:S(2)}) copy-start(s32[192]{0:T(256)} %param.17) | copy-start | bytes 2308
  0.7 1.0 %copy-start.8 = (f32[2,32,1]{1,2,0:T(1,128)S(1)}, f32[2,32,1]{1,2,0:T(1,128)}, u32[]{:S(2)}) copy-start(f32[2,32,1]{1,2,0:T(1,128)} %param.21) | copy-start | bytes 772
  0.7 1.0 %copy-start.9 = (f32[2,32,1]{1,2,0:T(1,128)S(1)}, f32[2,32,1]{1,2,0:T(1,128)}, u32[]{:S(2)}) copy-start(f32[2,32,1]{1,2,0:T(1,128)} %param.23) | copy-start | bytes 772
  0.7 1.0 %copy-start.5 = (s32[256,1]{0,1:T(1,128)S(1)}, s32[256,1]{0,1:T(1,128)}, u32[]{:S(2)}) copy-start(s32[256,1]{0,1:T(1,128)} %param.15) | copy-start | bytes 3076
  0.7 1.0 %copy-start.10 = (s32[2]{0:T(128)S(1)}, s32[2]{0:T(128)}, u32[]{:S(2)}) copy-start(s32[2]{0:T(128)} %param.18) | copy-start | bytes 28
  68.0 4.6 %copy-start = (bf16[2,64,1024]{2,1,0:T(8,128)(2,1)S(1)}, bf16[2,64,1024]{2,1,0:T(8,128)(2,1)}, u32[]{:S(2)}) copy-start(bf16[2,64,1024]{2,1,0:T(8,128)(2,1)} %mc_ref.3) | copy-start | bytes 786436
  68.0 4.6 %copy-start.1 = (bf16[2,64,1024]{2,1,0:T(8,128)(2,1)S(1)}, bf16[2,64,1024]{2,1,0:T(8,128)(2,1)}, u32[]{:S(2)}) copy-start(bf16[2,64,1024]{2,1,0:T(8,128)(2,1)} %vc_ref.3) | copy-start | bytes 786436
  68.0 4.6 %copy-start.2 = (bf16[2,64,1024]{2,1,0:T(8,128)(2,1)S(1)}, bf16[2,64,1024]{2,1,0:T(8,128)(2,1)}, u32[]{:S(2)}) copy-start(bf16[2,64,1024]{2,1,0:T(8,128)(2,1)} %weight_ref.1) | copy-start | bytes 786436
  68.7 3.8 %collective-permute-start = (f32[128,1024]{1,0:T(8,128)S(1)}, f32[128,1024]{1,0:T(8,128)S(1)}, u32[]{:S(2)}, u32[]{:S(2)}) collective-permute-start(f32[128,1024]{1,0:T(8,128)S(1)} %get-tuple-element.112), channel_id=1, source_target_pairs={{0,4},{4,0},{1,5},{5,1},{2,6},{6,2},{3,7},{7,3},{8,12},{12,8},{9,1... | collective-permute-start | bytes 1572872 | tf_op jit(solution)/shard_map/ppermute | solution.py:363
  74.0 19.9 %all-to-all-start.2 = ((bf16[4,2,64,1024]{3,2,1,0:T(8,128)(2,1)}), bf16[4,2,64,1024]{3,2,1,0:T(8,128)(2,1)S(1)}, u32[]{:S(2)}, u32[]{:S(2)}) async-start(bf16[4,2,64,1024]{3,2,1,0:T(8,128)(2,1)} %get-tuple-element.119), calls=%async_computation.2 | async-start | bytes 2097152 | tf_op jit(solution)/shard_map/all_to_all | solution.py:365
